TPU v7x, 32 devices: a whole 2x2x4 slice. The times are simulated.
32 devices in a mesh: ctx: 4 (over z), kvh: 4 (over y, x), conv: 2 (over core).
Axes of the slice: x: 2, y: 2, z: 4, core: 2. Of those that a mesh axis runs over, the one named last changes fastest.
Arguments:
- queries: bfloat16 [2, 512, 64, 128], P('conv', 'ctx', 'kvh'), may hold values from -6 to 6
- keys: bfloat16 [2, 4096, 8, 128], P('conv', 'ctx', 'kvh'), may hold values from -6 to 6
- values: bfloat16 [2, 4096, 8, 128], P('conv', 'ctx', 'kvh'), may hold values from -6 to 6
- lengths: int32 [2], P('conv'), may hold values from 64 to 3584
Outputs:
- attended: bfloat16 [2, 512, 64, 128], P('conv', 'ctx', 'kvh')
Inputs may be any that keep to these rules, and one draw needn't show every extreme that they name: The new turn's keys and values stand at cache positions lengths to lengths + 511; later positions hold unused entries.
All inputs are finite; a program needn't handle non-finite values.
Results may differ from a plain program's by a relative error of at most 0.005.
Values may be sent and summed in bfloat16 or wider, within the bound.
No kernel may reach another device: no remote copies, remote signals or barrier semaphores. Data moves between devices by JAX's collectives and lax.ppermute only.
A program may use at most 64 MiB of HBM per device.

v0:
```python
import jax
import jax.numpy as jnp
from jax import lax
from jax.sharding import PartitionSpec as P

mask_fill = -1e30


def shards(queries, keys, values, lengths):
    conv_dev, tok_dev, head_dev, head_dim = queries.shape
    ctx_dev = keys.shape[1]
    kv_dev = keys.shape[2]
    group_size = head_dev // kv_dev
    cycle_size = lax.axis_size("ctx")
    score_scale = 1.0 / head_dim**0.5
    key_position = lax.axis_index("ctx") * ctx_dev + jnp.arange(ctx_dev, dtype=jnp.int32)
    piece_rows = lax.all_gather(queries, "ctx", axis=1, tiled=True)
    row_count = piece_rows.shape[1]
    block_size = 64
    block_total = row_count // block_size
    blocks = jnp.moveaxis(
        piece_rows.reshape(conv_dev, block_total, block_size, head_dev, head_dim), 1, 0
    )

    def one_block(block_args):
        query_block, block_index = block_args
        query_block = query_block.reshape(conv_dev, block_size, kv_dev, group_size, head_dim)
        scores = (
            jnp.einsum("cbkgd,cskd->ckbgs", query_block, keys, preferred_element_type=jnp.float32)
            * score_scale
        )
        query_position = (
            lengths[:, None]
            + block_index * block_size
            + jnp.arange(block_size, dtype=jnp.int32)[None, :]
        )
        visible = key_position[None, None, None, None, :] <= query_position[:, None, :, None, None]
        masked = jnp.where(visible, scores, mask_fill)
        row_max = jnp.max(masked, axis=-1)
        weights = jnp.where(visible, jnp.exp(masked - row_max[..., None]), 0.0)
        exp_total = jnp.sum(weights, axis=-1)
        rounded = weights.astype(jnp.bfloat16)
        weighted = jnp.einsum(
            "ckbgs,cskd->ckbgd", rounded, values, preferred_element_type=jnp.float32
        )
        safe_total = jnp.maximum(exp_total, 1.0)
        partial_value = (weighted / safe_total[..., None]).astype(jnp.bfloat16)
        log_total = row_max + jnp.log(safe_total)
        partial_value = jnp.transpose(partial_value, (0, 2, 1, 3, 4)).reshape(
            conv_dev, block_size, head_dev, head_dim
        )
        log_total = jnp.transpose(log_total, (0, 2, 1, 3)).reshape(conv_dev, block_size, head_dev)
        return (partial_value, log_total)

    partial_value, log_total = lax.map(
        one_block, (blocks, jnp.arange(block_total, dtype=jnp.int32))
    )
    partial_value = jnp.moveaxis(partial_value, 0, 1).reshape(
        conv_dev, row_count, head_dev, head_dim
    )
    log_total = jnp.moveaxis(log_total, 0, 1).reshape(conv_dev, row_count, head_dev)
    partial_value, log_total = (partial_value, log_total)
    arrived = lax.all_to_all(
        partial_value.reshape(conv_dev, cycle_size, tok_dev, head_dev, head_dim),
        "ctx",
        split_axis=1,
        concat_axis=1,
        tiled=True,
    )
    arrived_totals = lax.all_to_all(
        log_total.reshape(conv_dev, cycle_size, tok_dev, head_dev),
        "ctx",
        split_axis=1,
        concat_axis=1,
        tiled=True,
    )
    top = jnp.max(arrived_totals, axis=1)
    share = jnp.exp(arrived_totals - top[:, None])
    numerator = jnp.sum(share[..., None] * arrived.astype(jnp.float32), axis=1)
    denominator = jnp.sum(share, axis=1)
    return (numerator / denominator[..., None]).astype(jnp.bfloat16)


def solution(mesh):
    in_specs = (
        P("conv", "ctx", "kvh", None),
        P("conv", "ctx", "kvh", None),
        P("conv", "ctx", "kvh", None),
        P("conv"),
    )
    out_specs = P("conv", "ctx", "kvh", None)
    return jax.shard_map(shards, mesh=mesh, in_specs=in_specs, out_specs=out_specs, check_vma=False)
```

profile of v0, /device:TPU:0, one launch (start us, length us, event | category | flops | bytes accessed | tf_op | source)
XLA Modules:
  0.0 183.0 jit_solution(16355917170916339926)
XLA Ops:
  6.5 0.7 all-gather.2.cloned.1.call-update
  7.3 1.1 copy.20
  8.4 1.1 copy.21
  9.5 47.8 %all-gather.2.cloned.1.call-done = bf16[1,512,16,128]{3,2,0,1:T(8,128)(2,1)} async-done(((bf16[1,128,16,128]{3,2,0,1:T(8,128)(2,1)}), bf16[1,512,16,128]{3,2,0,1:T(8,128)(2,1)}) %all-gather.2.cloned.1.call-update) | async-done | bytes 2097168 | tf_op jit(solution)/shard_map/all_gather | solution.py:17
  57.3 57.1 %while.13 = (s32[]{:T(128)}, bf16[8,1,64,16,128]{4,3,2,1,0:T(8,128)(2,1)S(1)}, f32[8,1,64,16]{2,0,3,1:T(8,128)S(1)}, s32[8]{0:T(128)S(1)}, s32[1]{0:T(128)}, /*i...) while((s32[]{:T(128)}, ...), condition=%wide.region_3.4_spmd.clone, body=%wide.region_0.3_spmd.clone.sunk | while | flops 550831168 | bytes 15004841 | solution.py:55
  57.3 0.6 dynamic_slice.16
  59.2 0.1 broadcast_compare_fusion.2
  59.3 2.1 %fusion.34 = (f32[2,64,8]{2,1,0:T(8,128)S(1)}, f32[2,64,8,1024]{3,2,1,0:T(8,128)S(1)}) fusion(pred[64,1024]{1,0:T(8,128)(4,1)S(1)} %broadcast_compare_fusion.2, bf16[1,1024,2,128]{3,1,2,0:T(8,128)(2,1)S(1)} %get-tuple-element.220, bf16[8,1,64,16,128]{4,3,2,1,0:T(8,128)(2,1)} %get-tuple-element.219, s32[]{:T(128)} %get-tuple-element.202), kind=kOutput, calls=%fused_computation.3.clone.1 | convolution fusion | flops 271580160 | bytes 5050880 | tf_op jit(solution)/shard_map/while/body/eval_jaxpr/cbkgd,cskd->ckbgs/dot_general | solution.py:29
  61.4 1.5 fusion.35
  62.9 1.3 fusion.36
  64.3 0.1 bitcast_dynamic-update-slice_fusion.2
  64.5 0.6 dynamic_slice.16
  66.4 0.1 broadcast_compare_fusion.2
  66.5 2.1 %fusion.34 = (f32[2,64,8]{2,1,0:T(8,128)S(1)}, f32[2,64,8,1024]{3,2,1,0:T(8,128)S(1)}) fusion(pred[64,1024]{1,0:T(8,128)(4,1)S(1)} %broadcast_compare_fusion.2, bf16[1,1024,2,128]{3,1,2,0:T(8,128)(2,1)S(1)} %get-tuple-element.220, bf16[8,1,64,16,128]{4,3,2,1,0:T(8,128)(2,1)} %get-tuple-element.219, s32[]{:T(128)} %get-tuple-element.202), kind=kOutput, calls=%fused_computation.3.clone.1 | convolution fusion | flops 271580160 | bytes 5050880 | tf_op jit(solution)/shard_map/while/body/eval_jaxpr/cbkgd,cskd->ckbgs/dot_general | solution.py:29
  68.6 1.5 fusion.35
  70.1 1.3 fusion.36
  71.4 0.1 bitcast_dynamic-update-slice_fusion.2
  71.6 0.6 dynamic_slice.16
  73.5 0.1 broadcast_compare_fusion.2
  73.6 2.1 %fusion.34 = (f32[2,64,8]{2,1,0:T(8,128)S(1)}, f32[2,64,8,1024]{3,2,1,0:T(8,128)S(1)}) fusion(pred[64,1024]{1,0:T(8,128)(4,1)S(1)} %broadcast_compare_fusion.2, bf16[1,1024,2,128]{3,1,2,0:T(8,128)(2,1)S(1)} %get-tuple-element.220, bf16[8,1,64,16,128]{4,3,2,1,0:T(8,128)(2,1)} %get-tuple-element.219, s32[]{:T(128)} %get-tuple-element.202), kind=kOutput, calls=%fused_computation.3.clone.1 | convolution fusion | flops 271580160 | bytes 5050880 | tf_op jit(solution)/shard_map/while/body/eval_jaxpr/cbkgd,cskd->ckbgs/dot_general | solution.py:29
  75.7 1.5 fusion.35
  77.2 1.3 fusion.36
  78.5 0.1 bitcast_dynamic-update-slice_fusion.2
  78.6 0.1 copy.44
  78.7 0.6 dynamic_slice.16
  80.6 0.1 broadcast_compare_fusion.2
  80.8 2.1 %fusion.34 = (f32[2,64,8]{2,1,0:T(8,128)S(1)}, f32[2,64,8,1024]{3,2,1,0:T(8,128)S(1)}) fusion(pred[64,1024]{1,0:T(8,128)(4,1)S(1)} %broadcast_compare_fusion.2, bf16[1,1024,2,128]{3,1,2,0:T(8,128)(2,1)S(1)} %get-tuple-element.220, bf16[8,1,64,16,128]{4,3,2,1,0:T(8,128)(2,1)} %get-tuple-element.219, s32[]{:T(128)} %get-tuple-element.202), kind=kOutput, calls=%fused_computation.3.clone.1 | convolution fusion | flops 271580160 | bytes 5050880 | tf_op jit(solution)/shard_map/while/body/eval_jaxpr/cbkgd,cskd->ckbgs/dot_general | solution.py:29
  82.9 1.5 fusion.35
  84.4 1.3 fusion.36
  85.7 0.1 bitcast_dynamic-update-slice_fusion.2
  85.9 0.6 dynamic_slice.16
  87.8 0.1 broadcast_compare_fusion.2
  87.9 2.1 %fusion.34 = (f32[2,64,8]{2,1,0:T(8,128)S(1)}, f32[2,64,8,1024]{3,2,1,0:T(8,128)S(1)}) fusion(pred[64,1024]{1,0:T(8,128)(4,1)S(1)} %broadcast_compare_fusion.2, bf16[1,1024,2,128]{3,1,2,0:T(8,128)(2,1)S(1)} %get-tuple-element.220, bf16[8,1,64,16,128]{4,3,2,1,0:T(8,128)(2,1)} %get-tuple-element.219, s32[]{:T(128)} %get-tuple-element.202), kind=kOutput, calls=%fused_computation.3.clone.1 | convolution fusion | flops 271580160 | bytes 5050880 | tf_op jit(solution)/shard_map/while/body/eval_jaxpr/cbkgd,cskd->ckbgs/dot_general | solution.py:29
  90.0 1.5 fusion.35
  91.5 1.3 fusion.36
  92.8 0.1 bitcast_dynamic-update-slice_fusion.2
  92.9 0.1 copy.44
  93.0 0.6 dynamic_slice.16
  94.9 0.1 broadcast_compare_fusion.2
  95.0 2.1 %fusion.34 = (f32[2,64,8]{2,1,0:T(8,128)S(1)}, f32[2,64,8,1024]{3,2,1,0:T(8,128)S(1)}) fusion(pred[64,1024]{1,0:T(8,128)(4,1)S(1)} %broadcast_compare_fusion.2, bf16[1,1024,2,128]{3,1,2,0:T(8,128)(2,1)S(1)} %get-tuple-element.220, bf16[8,1,64,16,128]{4,3,2,1,0:T(8,128)(2,1)} %get-tuple-element.219, s32[]{:T(128)} %get-tuple-element.202), kind=kOutput, calls=%fused_computation.3.clone.1 | convolution fusion | flops 271580160 | bytes 5050880 | tf_op jit(solution)/shard_map/while/body/eval_jaxpr/cbkgd,cskd->ckbgs/dot_general | solution.py:29
  97.1 1.5 fusion.35
  98.6 1.3 fusion.36
  100.0 0.1 bitcast_dynamic-update-slice_fusion.2
  100.0 0.1 copy.44
  100.2 0.6 dynamic_slice.16
  102.1 0.1 broadcast_compare_fusion.2
  102.2 2.1 %fusion.34 = (f32[2,64,8]{2,1,0:T(8,128)S(1)}, f32[2,64,8,1024]{3,2,1,0:T(8,128)S(1)}) fusion(pred[64,1024]{1,0:T(8,128)(4,1)S(1)} %broadcast_compare_fusion.2, bf16[1,1024,2,128]{3,1,2,0:T(8,128)(2,1)S(1)} %get-tuple-element.220, bf16[8,1,64,16,128]{4,3,2,1,0:T(8,128)(2,1)} %get-tuple-element.219, s32[]{:T(128)} %get-tuple-element.202), kind=kOutput, calls=%fused_computation.3.clone.1 | convolution fusion | flops 271580160 | bytes 5050880 | tf_op jit(solution)/shard_map/while/body/eval_jaxpr/cbkgd,cskd->ckbgs/dot_general | solution.py:29
  104.3 1.5 fusion.35
  105.8 1.3 fusion.36
  107.1 0.1 bitcast_dynamic-update-slice_fusion.2
  107.3 0.6 dynamic_slice.16
  109.2 0.1 broadcast_compare_fusion.2
  109.3 2.1 %fusion.34 = (f32[2,64,8]{2,1,0:T(8,128)S(1)}, f32[2,64,8,1024]{3,2,1,0:T(8,128)S(1)}) fusion(pred[64,1024]{1,0:T(8,128)(4,1)S(1)} %broadcast_compare_fusion.2, bf16[1,1024,2,128]{3,1,2,0:T(8,128)(2,1)S(1)} %get-tuple-element.220, bf16[8,1,64,16,128]{4,3,2,1,0:T(8,128)(2,1)} %get-tuple-element.219, s32[]{:T(128)} %get-tuple-element.202), kind=kOutput, calls=%fused_computation.3.clone.1 | convolution fusion | flops 271580160 | bytes 5050880 | tf_op jit(solution)/shard_map/while/body/eval_jaxpr/cbkgd,cskd->ckbgs/dot_general | solution.py:29
  111.4 1.5 fusion.35
  112.9 1.3 fusion.36
  114.3 0.1 bitcast_dynamic-update-slice_fusion.2
  114.5 0.1 reshape_reshape_transpose.6
  114.6 8.1 %all_to_all.10 = f32[1,4,128,16]{2,3,0,1:T(8,128)S(1)} all-to-all(f32[1,4,128,16]{2,3,0,1:T(8,128)S(1)} %copy.23), channel_id=1, replica_groups=mesh['ctx'=4,'kvh'=4,'conv'=2] {'ctx'}, dimensions={1} | all-to-all | bytes 65536 | tf_op jit(solution)/shard_map/all_to_all | solution.py:70
  122.7 3.6 %all-to-all-start.1 = ((bf16[1,4,128,16,128]{4,3,2,0,1:T(8,128)(2,1)}), bf16[1,4,128,16,128]{4,3,2,0,1:T(8,128)(2,1)S(1)}, u32[]{:S(2)}, u32[]{:S(2)}) async-start(bf16[1,4,128,16,128]{4,3,2,0,1:T(8,128)(2,1)} %bitcast.63), calls=%async_computation.1 | async-start | bytes 4194304 | tf_op jit(solution)/shard_map/all_to_all | solution.py:63
  126.3 0.1 copy.24
  126.5 0.1 copy.26
  126.6 46.9 %all-to-all-done.1 = bf16[1,4,128,16,128]{4,3,2,0,1:T(8,128)(2,1)S(1)} async-done(((bf16[1,4,128,16,128]{4,3,2,0,1:T(8,128)(2,1)}), bf16[1,4,128,16,128]{4,3,2,0,1:T(8,128)(2,1)S(1)}, u32[]{:S(2)}, u32[]{:S(2)}) %all-to-all-start.1) | async-done | bytes 2097184 | tf_op jit(solution)/shard_map/all_to_all | solution.py:63
  173.5 1.5 multiply_reduce_fusion
  175.0 1.1 fusion.24
  (46 shorter events, 0.9 us)
Async XLA Ops:
  6.5 50.8 %all-gather.2.cloned.1.call-start = ((), (), s32[]{:S(2)}) async-start(), calls=%async_computation.2 | async-start | bytes 2621440 | tf_op jit(solution)/shard_map/all_gather | solution.py:17
  114.5 8.2 %copy-start = (bf16[8,1,64,16,128]{4,3,2,1,0:T(8,128)(2,1)}, bf16[8,1,64,16,128]{4,3,2,1,0:T(8,128)(2,1)S(1)}, u32[]{:S(2)}) copy-start(bf16[8,1,64,16,128]{4,3,2,1,0:T(8,128)(2,1)S(1)} %get-tuple-element.54) | copy-start | bytes 6291460
  122.7 50.8 %all-to-all-start.1 = ((bf16[1,4,128,16,128]{4,3,2,0,1:T(8,128)(2,1)}), bf16[1,4,128,16,128]{4,3,2,0,1:T(8,128)(2,1)S(1)}, u32[]{:S(2)}, u32[]{:S(2)}) async-start(bf16[1,4,128,16,128]{4,3,2,0,1:T(8,128)(2,1)} %bitcast.63), calls=%async_computation.1 | async-start | bytes 4194304 | tf_op jit(solution)/shard_map/all_to_all | solution.py:63
Sparse Core Ops, SparseCore 0:
  8.9 48.3 all-gather.1
where the time goes:
time: 184 us; the launch traced here: 183 us
  waiting for transfers between devices  95.4 us (52%)
  matrix products  27.3 us (15%)
  other arithmetic  15.6 us (8%)
  between operations  13.5 us (7%)
  loops' own time  10.6 us (6%)
  local copies, waits for them, and re-layouts  8.89 us (5%)
  blocking collectives  8.11 us (4%)
  starting transfers between devices  3.61 us (2%)
    all_gather x1, waiting for transfers between devices, shards(): piece_rows = lax.all_gather(queries, 'ctx', axis=1, tiled=True)  47.8 us
    all_to_all x1, waiting for transfers between devices, shards(): lax.all_to_all(partial_value.reshape(conv_dev, cycle_size, tok_dev, head_...  46.9 us
    dot_general x8, matrix products, one_block(): jnp.einsum('cbkgd,cskd->ckbgs', query_block, keys, preferred_element_type...  16.8 us
    reduce_sum x8, other arithmetic, one_block(): exp_total = jnp.sum(weights, axis=-1)  11.8 us
    another operation x1, loops' own time, shards(): lax.map(one_block, (blocks, jnp.arange(block_total, dtype=jnp.int32)))  10.6 us
    dot_general x8, matrix products, one_block(): jnp.einsum('ckbgs,cskd->ckbgd', rounded, values, preferred_element_type=j...  10.5 us
    all_to_all x1, blocking collectives, shards(): lax.all_to_all(log_total.reshape(conv_dev, cycle_size, tok_dev, head_dev)...  8.11 us
    dynamic_slice x8, local copies, waits for them, and re-layouts, shards(): lax.map(one_block, (blocks, jnp.arange(block_total, dtype=jnp.int32)))  4.94 us
  transfers between devices with their start and end apart: 2, of which 2 were waited for; matrix products, arithmetic and copies ran while one was open for 1% of the time, Pallas kernels for 0%

commit v1 on v0

--- a/solution.py
+++ b/solution.py
@@ -4,6 +4,16 @@
 from jax.sharding import PartitionSpec as P
 
 mask_fill = -1e30
+
+
+def turned_line(x, name, dim):
+    devices = lax.axis_size(name)
+    held, blocks = (x, [x])
+    for _ in range(devices - 1):
+        held = lax.ppermute(held, name, [(i, (i + 1) % devices) for i in range(devices)])
+        blocks.insert(0, held)
+    merged = jnp.concatenate(blocks, axis=dim)
+    return jnp.roll(merged, (lax.axis_index(name) + 1) * x.shape[dim], axis=dim)
 
 
 def shards(queries, keys, values, lengths):
@@ -14,7 +24,7 @@
     cycle_size = lax.axis_size("ctx")
     score_scale = 1.0 / head_dim**0.5
     key_position = lax.axis_index("ctx") * ctx_dev + jnp.arange(ctx_dev, dtype=jnp.int32)
-    piece_rows = lax.all_gather(queries, "ctx", axis=1, tiled=True)
+    piece_rows = turned_line(queries, "ctx", 1)
     row_count = piece_rows.shape[1]
     block_size = 64
     block_total = row_count // block_size

time: 184 us -> 162 us (0.88)
  between operations: 13.5 us -> 0.16 us
  waiting for transfers between devices: 95.4 us -> 85.6 us
  matrix products: 27.3 us -> 19.7 us
  local copies, waits for them, and re-layouts: 8.89 us -> 15.3 us
  starting transfers between devices: 3.61 us -> 6.66 us
    all_gather x1 -> x0, waiting for transfers between devices: 47.8 us -> none  [shards(): piece_rows = lax.all_gather(queries, 'ctx', axis=1, tiled=True)]
    ppermute x0 -> x3, waiting for transfers between devices: none -> 40.9 us  [turned_line(): lax.ppermute(held, name, [(i, (i + 1) % devices) for i in range(devices)])]
    dot_general x8, matrix products: 16.8 us -> 9.16 us  [one_block(): jnp.einsum('cbkgd,cskd->ckbgs', query_block, keys, preferred_element_type...]
    dynamic_update_slice x16, local copies, waits for them, and re-layouts: 0.9 us -> 6.41 us  [shards(): lax.map(one_block, (blocks, jnp.arange(block_total, dtype=jnp.int32)))]
    ppermute x0 -> x3, starting transfers between devices: none -> 3.06 us  [turned_line(): lax.ppermute(held, name, [(i, (i + 1) % devices) for i in range(devices)])]
    all_to_all x1, waiting for transfers between devices: 46.9 us -> 44.7 us  [shards(): lax.all_to_all(partial_value.reshape(conv_dev, cycle_size, tok_dev, head_...]
  transfers between devices with their start and end apart: 2 -> 4, of which waited for: 2 -> 4; matrix products, arithmetic and copies ran while one was open for 1% -> 2% of each run, Pallas kernels for 0% -> 0%
where the time goes in v1:
time: 162 us
  waiting for transfers between devices  85.6 us (53%)
  matrix products  19.7 us (12%)
  other arithmetic  15.5 us (10%)
  local copies, waits for them, and re-layouts  15.3 us (9%)
  loops' own time  10.6 us (7%)
  blocking collectives  8.01 us (5%)
  starting transfers between devices  6.66 us (4%)
    all_to_all x1, waiting for transfers between devices, shards(): lax.all_to_all(partial_value.reshape(conv_dev, cycle_size, tok_dev, head_...  44.7 us
    ppermute x3, waiting for transfers between devices, turned_line(): lax.ppermute(held, name, [(i, (i + 1) % devices) for i in range(devices)])  40.9 us
    reduce_sum x8, other arithmetic, one_block(): exp_total = jnp.sum(weights, axis=-1)  11.8 us
    another operation x1, loops' own time, shards(): lax.map(one_block, (blocks, jnp.arange(block_total, dtype=jnp.int32)))  10.6 us
    dot_general x8, matrix products, one_block(): jnp.einsum('ckbgs,cskd->ckbgd', rounded, values, preferred_element_type=j...  10.5 us
    dot_general x8, matrix products, one_block(): jnp.einsum('cbkgd,cskd->ckbgs', query_block, keys, preferred_element_type...  9.16 us
    all_to_all x1, blocking collectives, shards(): lax.all_to_all(log_total.reshape(conv_dev, cycle_size, tok_dev, head_dev)...  8.01 us
    dynamic_update_slice x16, local copies, waits for them, and re-layouts, shards(): lax.map(one_block, (blocks, jnp.arange(block_total, dtype=jnp.int32)))  6.41 us
  transfers between devices with their start and end apart: 4, of which 4 were waited for; matrix products, arithmetic and copies ran while one was open for 2% of the time, Pallas kernels for 0%

profile of v1, /device:TPU:0, one launch (start us, length us, event | category | flops | bytes accessed | tf_op | source)
XLA Modules:
  0.0 161.6 jit_solution(10022397274347340649)
XLA Ops:
  0.0 3.1 %collective-permute-start = (bf16[1,128,16,128]{3,2,1,0:T(8,128)(2,1)}, bf16[1,128,16,128]{3,2,1,0:T(8,128)(2,1)S(1)}, u32[]{:S(2)}, u32[]{:S(2)}) collective-permute-start(bf16[1,128,16,128]{3,2,1,0:T(8,128)(2,1)} %param.6), channel_id=1, source_target_pairs={{0,8},{8,16},{16,24},{24,0},{1,9},{9,17},{17,25},{25,1},{2,10},{10... | collective-permute-start | bytes 1572872 | tf_op jit(solution)/shard_map/ppermute | solution.py:13
  3.1 14.2 %collective-permute-done = bf16[1,128,16,128]{3,2,1,0:T(8,128)(2,1)S(1)} collective-permute-done((bf16[1,128,16,128]{3,2,1,0:T(8,128)(2,1)}, bf16[1,128,16,128]{3,2,1,0:T(8,128)(2,1)S(1)}, u32[]{:S(2)}, u32[]{:S(2)}) %collective-permute-start) | collective-permute-done | bytes 524320 | tf_op jit(solution)/shard_map/ppermute | solution.py:13
  17.3 14.9 %collective-permute-done.1 = bf16[1,128,16,128]{3,2,1,0:T(8,128)(2,1)S(1)} collective-permute-done((bf16[1,128,16,128]{3,2,1,0:T(8,128)(2,1)S(1)}, bf16[1,128,16,128]{3,2,1,0:T(8,128)(2,1)S(1)}, u32[]{:S(2)}, u32[]{:S(2)}) %collective-permute-start.1) | collective-permute-done | bytes 524320 | tf_op jit(solution)/shard_map/ppermute | solution.py:13
  32.2 1.1 copy.18
  33.3 1.1 copy.19
  34.4 11.8 %collective-permute-done.2 = bf16[1,128,16,128]{3,2,1,0:T(8,128)(2,1)S(1)} collective-permute-done((bf16[1,128,16,128]{3,2,1,0:T(8,128)(2,1)S(1)}, bf16[1,128,16,128]{3,2,1,0:T(8,128)(2,1)S(1)}, u32[]{:S(2)}, u32[]{:S(2)}) %collective-permute-start.2) | collective-permute-done | bytes 524320 | tf_op jit(solution)/shard_map/ppermute | solution.py:13
  46.8 0.4 constant_dynamic-slice_fusion
  47.2 54.9 %while.13 = (s32[]{:T(128)}, bf16[8,1,64,16,128]{4,3,2,1,0:T(8,128)(2,1)}, f32[8,1,64,16]{2,0,3,1:T(8,128)S(1)}, s32[8]{0:T(128)S(1)}, s32[1]{0:T(128)}, /*index...) while((s32[]{:T(128)}, ...), condition=%wide.region_3.4_spmd.clone, body=%wide.region_0.3_spmd.clone.sunk | while | flops 550831168 | bytes 15004841 | solution.py:65
  47.2 0.6 dynamic_slice.22
  49.1 0.1 broadcast_compare_fusion.2
  49.2 1.1 fusion.34
  50.4 1.5 fusion.35
  51.9 1.3 fusion.36
  53.2 0.7 bitcast_dynamic-update-slice_fusion.2
  54.0 0.6 dynamic_slice.22
  55.9 0.1 broadcast_compare_fusion.2
  56.1 1.1 fusion.34
  57.2 1.5 fusion.35
  58.7 1.3 fusion.36
  60.0 0.8 bitcast_dynamic-update-slice_fusion.2
  60.9 0.6 dynamic_slice.22
  62.8 0.1 broadcast_compare_fusion.2
  62.9 1.1 fusion.34
  64.1 1.5 fusion.35
  65.6 1.3 fusion.36
  66.9 0.8 bitcast_dynamic-update-slice_fusion.2
  67.8 0.6 dynamic_slice.22
  69.7 0.1 broadcast_compare_fusion.2
  69.8 1.1 fusion.34
  70.9 1.5 fusion.35
  72.4 1.3 fusion.36
  73.8 0.8 bitcast_dynamic-update-slice_fusion.2
  74.6 0.6 dynamic_slice.22
  76.5 0.1 broadcast_compare_fusion.2
  76.7 1.1 fusion.34
  77.8 1.5 fusion.35
  79.3 1.3 fusion.36
  80.6 0.8 bitcast_dynamic-update-slice_fusion.2
  81.5 0.6 dynamic_slice.22
  83.4 0.1 broadcast_compare_fusion.2
  83.5 1.1 fusion.34
  84.7 1.5 fusion.35
  86.2 1.3 fusion.36
  87.5 0.8 bitcast_dynamic-update-slice_fusion.2
  88.4 0.6 dynamic_slice.22
  90.3 0.1 broadcast_compare_fusion.2
  90.4 1.1 fusion.34
  91.6 1.5 fusion.35
  93.1 1.3 fusion.36
  94.4 0.8 bitcast_dynamic-update-slice_fusion.2
  95.3 0.6 dynamic_slice.22
  97.2 0.1 broadcast_compare_fusion.2
  97.3 1.1 fusion.34
  98.4 1.5 fusion.35
  99.9 1.3 fusion.36
  101.2 0.8 bitcast_dynamic-update-slice_fusion.2
  102.1 0.1 reshape_reshape_transpose.6
  102.2 8.0 %all_to_all.10 = f32[1,4,128,16]{2,3,0,1:T(8,128)S(1)} all-to-all(f32[1,4,128,16]{2,3,0,1:T(8,128)S(1)} %copy.21), channel_id=1, replica_groups=mesh['ctx'=4,'kvh'=4,'conv'=2] {'ctx'}, dimensions={1} | all-to-all | bytes 65536 | tf_op jit(solution)/shard_map/all_to_all | solution.py:80
  110.2 3.6 %all-to-all-start.1 = ((bf16[1,4,128,16,128]{4,3,2,0,1:T(8,128)(2,1)}), bf16[1,4,128,16,128]{4,3,2,0,1:T(8,128)(2,1)S(1)}, u32[]{:S(2)}, u32[]{:S(2)}) async-start(bf16[1,4,128,16,128]{4,3,2,0,1:T(8,128)(2,1)} %bitcast.61), calls=%async_computation.1 | async-start | bytes 4194304 | tf_op jit(solution)/shard_map/all_to_all | solution.py:73
  113.9 0.1 copy.22
  114.0 0.1 copy.24
  114.1 44.7 %all-to-all-done.1 = bf16[1,4,128,16,128]{4,3,2,0,1:T(8,128)(2,1)S(1)} async-done(((bf16[1,4,128,16,128]{4,3,2,0,1:T(8,128)(2,1)}), bf16[1,4,128,16,128]{4,3,2,0,1:T(8,128)(2,1)S(1)}, u32[]{:S(2)}, u32[]{:S(2)}) %all-to-all-start.1) | async-done | bytes 2097184 | tf_op jit(solution)/shard_map/all_to_all | solution.py:73
  158.9 1.5 multiply_reduce_fusion
  160.4 1.1 fusion.24
  (58 shorter events, 1.6 us)
Async XLA Ops:
  0.0 46.4 %copy-start = (bf16[1,128,16,128]{3,2,1,0:T(8,128)(2,1)S(1)}, bf16[1,128,16,128]{3,2,1,0:T(8,128)(2,1)}, u32[]{:S(2)}) copy-start(bf16[1,128,16,128]{3,2,1,0:T(8,128)(2,1)} %param.6) | copy-start | bytes 1572868
  0.0 17.3 %collective-permute-start = (bf16[1,128,16,128]{3,2,1,0:T(8,128)(2,1)}, bf16[1,128,16,128]{3,2,1,0:T(8,128)(2,1)S(1)}, u32[]{:S(2)}, u32[]{:S(2)}) collective-permute-start(bf16[1,128,16,128]{3,2,1,0:T(8,128)(2,1)} %param.6), channel_id=1, source_target_pairs={{0,8},{8,16},{16,24},{24,0},{1,9},{9,17},{17,25},{25,1},{2,10},{10... | collective-permute-start | bytes 1572872 | tf_op jit(solution)/shard_map/ppermute | solution.py:13
  17.3 14.9 %collective-permute-start.1 = (bf16[1,128,16,128]{3,2,1,0:T(8,128)(2,1)S(1)}, bf16[1,128,16,128]{3,2,1,0:T(8,128)(2,1)S(1)}, u32[]{:S(2)}, u32[]{:S(2)}) collective-permute-start(bf16[1,128,16,128]{3,2,1,0:T(8,128)(2,1)S(1)} %collective-permute-done), channel_id=1, source_target_pairs={{0,8},{8,16},{16,24},{24,0},{1,9},{9,17},{17,25},{25,1},{2,10},{10... | collective-permute-start | bytes 1572872 | tf_op jit(solution)/shard_map/ppermute | solution.py:13
  32.2 14.0 %collective-permute-start.2 = (bf16[1,128,16,128]{3,2,1,0:T(8,128)(2,1)S(1)}, bf16[1,128,16,128]{3,2,1,0:T(8,128)(2,1)S(1)}, u32[]{:S(2)}, u32[]{:S(2)}) collective-permute-start(bf16[1,128,16,128]{3,2,1,0:T(8,128)(2,1)S(1)} %collective-permute-done.1), channel_id=1, source_target_pairs={{0,8},{8,16},{16,24},{24,0},{1,9},{9,17},{17,25},{25,1},{2,10},{10... | collective-permute-start | bytes 1572872 | tf_op jit(solution)/shard_map/ppermute | solution.py:13
  110.2 48.6 %all-to-all-start.1 = ((bf16[1,4,128,16,128]{4,3,2,0,1:T(8,128)(2,1)}), bf16[1,4,128,16,128]{4,3,2,0,1:T(8,128)(2,1)S(1)}, u32[]{:S(2)}, u32[]{:S(2)}) async-start(bf16[1,4,128,16,128]{4,3,2,0,1:T(8,128)(2,1)} %bitcast.61), calls=%async_computation.1 | async-start | bytes 4194304 | tf_op jit(solution)/shard_map/all_to_all | solution.py:73
